TPU v7x, 32 devices: a whole 2x2x4 slice. The times are simulated.
32 devices in a mesh: seq: 4 (over y, x), seg: 4 (over z), head: 2 (over core).
Axes of the slice: x: 2, y: 2, z: 4, core: 2. Of those that a mesh axis runs over, the one named last changes fastest.
Arguments:
- queries: bfloat16 [8, 16384, 128], P('head', ('seg', 'seq')), may hold values from -6 to 6
- keys: bfloat16 [8, 16384, 128], P('head', ('seg', 'seq')), may hold values from -6 to 6
- values: bfloat16 [8, 16384, 128], P('head', ('seg', 'seq')), may hold values from -8 to 8
- teacher: bfloat16 [8, 16384, 128], P('head', ('seg', 'seq')), may hold values from -6 to 6
- query_proj: float32 [128, 16], replicated, may hold values from -0.5 to 0.5
- key_proj: float32 [128, 16], replicated, may hold values from -0.5 to 0.5
Outputs:
- student: bfloat16 [8, 16384, 128], P('head', ('seg', 'seq'))
- query_grad: float32 [128, 16], replicated
- key_grad: float32 [128, 16], replicated
All inputs are finite; a program needn't handle non-finite values.
Results may differ from a plain program's by a relative error of at most 0.0014.
The roundings to bfloat16 on the way count: a program that leaves them out, or rounds other values in their place, can miss the bound.
Values sent between devices are 32-bit elements; how exact they have to be, the bound alone decides.
No kernel may reach another device: no remote copies, remote signals or barrier semaphores. Data moves between devices by JAX's collectives and lax.ppermute only.
A program may use at most 64 MiB of HBM per device.

v0:
```python
import math
import jax
import jax.numpy as jnp
import numpy as np
from jax import lax
from jax.sharding import PartitionSpec as P

highest = lax.Precision.HIGHEST


def carried_in(value, axis, join, neutral, backward):
    count, mine = (lax.axis_size(axis), lax.axis_index(axis))
    pieces = jax.tree.map(lambda part: lax.all_gather(part, axis), value)
    if backward:
        pieces = jax.tree.map(lambda part: part[::-1], pieces)
        mine = count - 1 - mine
    running = jax.tree.map(
        lambda part, zero: jnp.full_like(part, 0) + jnp.asarray(zero, part.dtype), value, neutral
    )

    def step(position, running):
        longer = join(running, jax.tree.map(lambda part: part[position], pieces))
        return jax.tree.map(lambda new, old: jnp.where(position < mine, new, old), longer, running)

    return lax.fori_loop(0, count - 1, step, running)


def feature_tables(width):
    first, second = np.triu_indices(width)
    eye = np.eye(width)
    coef = np.where(first == second, 0.5**0.5, 1.0)
    return (
        jnp.asarray(eye[first], jnp.float32),
        jnp.asarray(eye[second], jnp.float32),
        jnp.asarray(coef, jnp.float32),
    )


def features(proj_t, tables):
    sel_a, sel_b, coef = tables
    left = jnp.dot(sel_a, proj_t, precision=highest)
    right = jnp.dot(sel_b, proj_t, precision=highest)
    return jnp.concatenate([jnp.ones_like(proj_t[:1]), proj_t, coef[:, None] * left * right], 0)


def feature_grad(proj_t, grad_phi, tables):
    sel_a, sel_b, coef = tables
    width = proj_t.shape[0]
    left = jnp.dot(sel_a, proj_t, precision=highest)
    right = jnp.dot(sel_b, proj_t, precision=highest)
    quad = grad_phi[1 + width :] * coef[:, None]
    return (
        grad_phi[1 : 1 + width]
        + jnp.dot(sel_a.T, quad * right, precision=highest)
        + jnp.dot(sel_b.T, quad * left, precision=highest)
    )


def project(weight_b, rows):
    return lax.dot_general(
        weight_b, rows, (((0,), (1,)), ((), ())), preferred_element_type=jnp.float32
    )


def head_state(q_h, k_h, v_h, wq_b, wk_b, tables):
    q_t = project(wq_b, q_h)
    k_t = project(wk_b, k_h)
    phi_k = features(k_t, tables)
    state = jnp.dot(phi_k.astype(jnp.bfloat16), v_h, preferred_element_type=jnp.float32)
    return (q_t, k_t, state, jnp.sum(phi_k, 1))


def head_forward(q_t, k_t, v_h, teacher_h, s_prev, z_prev, scale, tables):
    phi_q = features(q_t, tables)
    length = q_t.shape[1]
    scores = lax.dot_general(q_t, k_t, (((0,), (0,)), ((), ())), precision=highest)
    causal = jnp.arange(length)[:, None] >= jnp.arange(length)[None, :]
    weights = jnp.where(causal, 1.0 + scores + 0.5 * scores * scores, 0.0)
    numer = jnp.dot(weights.astype(jnp.bfloat16), v_h, preferred_element_type=jnp.float32)
    numer = numer + lax.dot_general(phi_q, s_prev, (((0,), (0,)), ((), ())), precision=highest)
    denom = jnp.sum(weights, 1) + jnp.dot(z_prev, phi_q, precision=highest)
    student = numer / denom[:, None]
    g_out = scale * (student - teacher_h.astype(jnp.float32))
    g_numer = g_out / denom[:, None]
    g_denom = -jnp.sum(g_out * student, 1) / denom
    g_weights = (
        lax.dot_general(
            g_numer.astype(jnp.bfloat16),
            v_h,
            (((1,), (1,)), ((), ())),
            preferred_element_type=jnp.float32,
        )
        + g_denom[:, None]
    )
    g_scores = jnp.where(causal, g_weights * (1.0 + scores), 0.0)
    g_q = lax.dot_general(k_t, g_scores, (((1,), (1,)), ((), ())), precision=highest)
    g_k = jnp.dot(q_t, g_scores, precision=highest)
    g_phi_q = (
        lax.dot_general(s_prev, g_numer, (((1,), (1,)), ((), ())), precision=highest)
        + z_prev[:, None] * g_denom[None, :]
    )
    g_q = g_q + feature_grad(q_t, g_phi_q, tables)
    g_state = jnp.dot(phi_q, g_numer, precision=highest)
    h_state = jnp.dot(phi_q, g_denom, precision=highest)
    return (student, g_q, g_k, g_state, h_state)


def head_grads(q_h, k_h, v_h, k_t, g_q, g_k, g_next, h_next, tables):
    g_phi_k = (
        lax.dot_general(
            g_next.astype(jnp.bfloat16),
            v_h,
            (((1,), (1,)), ((), ())),
            preferred_element_type=jnp.float32,
        )
        + h_next[:, None]
    )
    g_k = g_k + feature_grad(k_t, g_phi_k, tables)
    grad_q = lax.dot_general(
        q_h, g_q.astype(jnp.bfloat16), (((0,), (1,)), ((), ())), preferred_element_type=jnp.float32
    )
    grad_k = lax.dot_general(
        k_h, g_k.astype(jnp.bfloat16), (((0,), (1,)), ((), ())), preferred_element_type=jnp.float32
    )
    return (grad_q, grad_k)


def add_trees(first, second):
    return jax.tree.map(jnp.add, first, second)


def masked_fold(mine, backward, carry, piece):
    rows = piece[0].shape[0]
    index = jnp.arange(rows)
    keep = index > mine if backward else index < mine

    def pick(array):
        shaped = keep.reshape((rows,) + (1,) * (array.ndim - 1))
        return jnp.sum(jnp.where(shaped, array, 0.0), 0)

    part = jax.tree.map(pick, piece)
    whole = jax.tree.map(lambda array: jnp.sum(array, 0), piece)
    return (add_trees(carry[0], part), add_trees(carry[1], whole))


def carried(local, backward):
    zeros = jax.tree.map(jnp.zeros_like, local)
    stacked = jax.tree.map(lambda array: array[None], local)
    inner, totals = masked_fold(
        lax.axis_index("seq"),
        backward,
        (zeros, zeros),
        (
            lax.all_gather(stacked[0], "seq", axis=0, tiled=True),
            lax.all_gather(stacked[1], "seq", axis=0, tiled=True),
        ),
    )
    outer = carried_in(totals, "seg", add_trees, zeros, backward)
    return add_trees(inner, outer)


def shards(queries, keys, values, teacher, query_proj, key_proj):
    tables = feature_tables(query_proj.shape[1])
    wq_b = query_proj.astype(jnp.bfloat16)
    wk_b = key_proj.astype(jnp.bfloat16)
    q_t, k_t, states, counts = lax.map(
        lambda xs: head_state(xs[0], xs[1], xs[2], wq_b, wk_b, tables), (queries, keys, values)
    )
    s_prev, z_prev = carried((states, counts), False)
    heads_all = queries.shape[0] * lax.axis_size("head")
    tokens_all = queries.shape[1] * lax.axis_size("seq") * lax.axis_size("seg")
    scale = 1.0 / math.sqrt(heads_all * tokens_all)
    student, g_q, g_k, g_state, h_state = lax.map(
        lambda xs: head_forward(xs[0], xs[1], xs[2], xs[3], xs[4], xs[5], scale, tables),
        (q_t, k_t, values, teacher, s_prev, z_prev),
    )
    g_next, h_next = carried((g_state, h_state), True)
    grad_q, grad_k = lax.map(
        lambda xs: head_grads(xs[0], xs[1], xs[2], xs[3], xs[4], xs[5], xs[6], xs[7], tables),
        (queries, keys, values, k_t, g_q, g_k, g_next, h_next),
    )
    summed = lax.psum((jnp.sum(grad_q, 0), jnp.sum(grad_k, 0)), ("seq", "seg", "head"))
    return (student.astype(jnp.bfloat16), summed[0], summed[1])


def solution(mesh):
    in_specs = (
        P("head", ("seg", "seq"), None),
        P("head", ("seg", "seq"), None),
        P("head", ("seg", "seq"), None),
        P("head", ("seg", "seq"), None),
        P(),
        P(),
    )
    out_specs = (P("head", ("seg", "seq"), None), P(), P())
    return jax.shard_map(shards, mesh=mesh, in_specs=in_specs, out_specs=out_specs, check_vma=False)
```

profile of v0, /device:TPU:0, one launch (start us, length us, event | category | flops | bytes accessed | tf_op | source)
XLA Modules:
  0.0 344.7 jit_solution(8274270570329167139)
XLA Ops:
  8.7 27.1 %while.81 = (s32[]{:T(128)}, f32[4,16,1024]{2,1,0:T(8,128)S(1)}, f32[4,16,1024]{2,1,0:T(8,128)S(1)}, f32[4,153,128]{2,1,0:T(8,128)S(1)}, f32[4,153]{1,0:T(4,128)...) while((s32[]{:T(128)}, f32[4,16,1024]{2,1,0:T(8,128)S(1)}, ...), condition=%wide.region_2.3_spmd.clone, body=%wide.region_0.2_spmd.sunk.clone.sunk | while | flops 103662440 | bytes 4145861 | solution.py:166
  11.0 1.5 convolution_multiply_fusion.7
  12.5 1.5 fusion.187
  13.9 1.3 fusion.188
  17.7 1.5 convolution_multiply_fusion.7
  19.2 1.5 fusion.187
  20.7 1.3 fusion.188
  24.5 1.5 convolution_multiply_fusion.7
  26.0 1.5 fusion.187
  27.5 1.3 fusion.188
  31.3 1.5 convolution_multiply_fusion.7
  32.8 1.5 fusion.187
  34.3 1.3 fusion.188
  36.6 31.5 %all-gather.17.cloned.1.call-done = f32[16,153,128]{2,1,0:T(8,128)} async-done(((f32[4,153,128]{2,1,0:T(8,128)}), f32[16,153,128]{2,1,0:T(8,128)}) %all-gather.17.cloned.1.call-update) | async-done | bytes 1253392 | tf_op jit(solution)/shard_map/all_gather | solution.py:154
  68.1 2.4 fusion.90
  70.6 8.1 %all-gather.8 = f32[4,4,153]{2,1,0:T(4,128)S(1)} all-gather(f32[1,4,153]{2,1,0:T(4,128)S(1)} %bitcast.304), channel_id=4, replica_groups=mesh['seq'=4,'seg'=4,'head'=2] {'seq'}, dimensions={0}, use_global_device_ids=true | all-gather | bytes 12240 | tf_op jit(solution)/shard_map/all_gather | solution.py:155
  78.8 13.7 %all-gather.9 = f32[4,4,153]{2,1,0:T(4,128)S(1)} all-gather(f32[1,4,153]{2,1,0:T(4,128)S(1)} %bitcast.301), channel_id=5, replica_groups=mesh['seq'=4,'seg'=4,'head'=2] {'seg'}, dimensions={0}, use_global_device_ids=true | all-gather | bytes 12240 | tf_op jit(solution)/shard_map/all_gather | solution.py:13
  93.2 10.2 %all-gather.19.cloned.1.call-done = f32[16,153,128]{2,1,0:T(8,128)} async-done(((f32[4,153,128]{2,1,0:T(8,128)}), f32[16,153,128]{2,1,0:T(8,128)}) %all-gather.19.cloned.1.call-update) | async-done | bytes 1253392 | tf_op jit(solution)/shard_map/all_gather | solution.py:13
  103.4 3.4 while.84
  109.1 98.5 %while.82 = (s32[]{:T(128)}, bf16[4,1024,128]{2,1,0:T(8,128)(2,1)}, bf16[4,16,1024]{2,1,0:T(8,128)(2,1)}, f32[4,16,1024]{2,1,0:T(8,128)}, f32[4,153,128]{2,1,0:T...) while((s32[]{:T(128)}, bf16[4,1024,128]{2,1,0:T(8,128)(2,1)}, ...), condition=%wide.region_12.13_spmd.clone, body=%wide.region_9.12_spmd.sunk.clone.sunk | while | flops 1998507008 | bytes 75882544 | solution.py:173
  110.4 3.8 %fusion.212 = (f32[1024]{0:T(1024)S(1)}, f32[1024,1024]{0,1:T(8,128)S(1)}) fusion(f32[16,1024]{1,0:T(8,128)S(1)} %dynamic-slice_bitcast_fusion.2, f32[4,16,1024]{2,1,0:T(8,128)S(1)} %get-tuple-element.1167, s32[]{:T(128)S(6)} %copy.77), kind=kOutput, calls=%fused_computation.28.clone.1 | convolution fusion | flops 208665600 | bytes 4329476 | tf_op jit(solution)/shard_map/while/body/eval_jaxpr/dot_general | solution.py:76
  116.0 1.6 fusion.215
  117.6 1.8 fusion.216
  120.3 2.1 convolution_add_fusion.13
  123.5 1.8 multiply_select_fusion.2
  125.3 2.1 fusion.217
  127.4 4.2 %fusion.218 = f32[4,16,1024]{2,1,0:T(8,128)} fusion(f32[4,16,1024]{2,1,0:T(8,128)} %get-tuple-element.1144, s32[]{:T(128)S(6)} %copy.77, f32[16,1024]{1,0:T(8,128)S(1)} %dynamic-slice_bitcast_fusion.2, f32[1024,1024]{0,1:T(8,128)S(1)} %multiply_select_fusion.2), kind=kOutput, calls=%fused_computation.37.clone.1 | convolution fusion | flops 201326592 | bytes 4325380 | tf_op jit(solution)/shard_map/while/body/eval_jaxpr/dot_general | solution.py:97
  131.6 1.4 fusion.219
  134.9 3.8 %fusion.212 = (f32[1024]{0:T(1024)S(1)}, f32[1024,1024]{0,1:T(8,128)S(1)}) fusion(f32[16,1024]{1,0:T(8,128)S(1)} %dynamic-slice_bitcast_fusion.2, f32[4,16,1024]{2,1,0:T(8,128)S(1)} %get-tuple-element.1167, s32[]{:T(128)S(6)} %copy.77), kind=kOutput, calls=%fused_computation.28.clone.1 | convolution fusion | flops 208665600 | bytes 4329476 | tf_op jit(solution)/shard_map/while/body/eval_jaxpr/dot_general | solution.py:76
  140.6 1.6 fusion.215
  142.2 1.8 fusion.216
  144.8 2.1 convolution_add_fusion.13
  148.0 1.8 multiply_select_fusion.2
  149.9 2.1 fusion.217
  152.0 4.2 %fusion.218 = f32[4,16,1024]{2,1,0:T(8,128)} fusion(f32[4,16,1024]{2,1,0:T(8,128)} %get-tuple-element.1144, s32[]{:T(128)S(6)} %copy.77, f32[16,1024]{1,0:T(8,128)S(1)} %dynamic-slice_bitcast_fusion.2, f32[1024,1024]{0,1:T(8,128)S(1)} %multiply_select_fusion.2), kind=kOutput, calls=%fused_computation.37.clone.1 | convolution fusion | flops 201326592 | bytes 4325380 | tf_op jit(solution)/shard_map/while/body/eval_jaxpr/dot_general | solution.py:97
  156.1 1.4 fusion.219
  159.5 3.8 %fusion.212 = (f32[1024]{0:T(1024)S(1)}, f32[1024,1024]{0,1:T(8,128)S(1)}) fusion(f32[16,1024]{1,0:T(8,128)S(1)} %dynamic-slice_bitcast_fusion.2, f32[4,16,1024]{2,1,0:T(8,128)S(1)} %get-tuple-element.1167, s32[]{:T(128)S(6)} %copy.77), kind=kOutput, calls=%fused_computation.28.clone.1 | convolution fusion | flops 208665600 | bytes 4329476 | tf_op jit(solution)/shard_map/while/body/eval_jaxpr/dot_general | solution.py:76
  165.1 1.6 fusion.215
  166.7 1.8 fusion.216
  169.4 2.1 convolution_add_fusion.13
  172.5 1.8 multiply_select_fusion.2
  174.4 2.1 fusion.217
  176.5 4.2 %fusion.218 = f32[4,16,1024]{2,1,0:T(8,128)} fusion(f32[4,16,1024]{2,1,0:T(8,128)} %get-tuple-element.1144, s32[]{:T(128)S(6)} %copy.77, f32[16,1024]{1,0:T(8,128)S(1)} %dynamic-slice_bitcast_fusion.2, f32[1024,1024]{0,1:T(8,128)S(1)} %multiply_select_fusion.2), kind=kOutput, calls=%fused_computation.37.clone.1 | convolution fusion | flops 201326592 | bytes 4325380 | tf_op jit(solution)/shard_map/while/body/eval_jaxpr/dot_general | solution.py:97
  180.7 1.4 fusion.219
  184.0 3.8 %fusion.212 = (f32[1024]{0:T(1024)S(1)}, f32[1024,1024]{0,1:T(8,128)S(1)}) fusion(f32[16,1024]{1,0:T(8,128)S(1)} %dynamic-slice_bitcast_fusion.2, f32[4,16,1024]{2,1,0:T(8,128)S(1)} %get-tuple-element.1167, s32[]{:T(128)S(6)} %copy.77), kind=kOutput, calls=%fused_computation.28.clone.1 | convolution fusion | flops 208665600 | bytes 4329476 | tf_op jit(solution)/shard_map/while/body/eval_jaxpr/dot_general | solution.py:76
  189.6 1.6 fusion.215
  191.2 1.8 fusion.216
  193.9 2.1 convolution_add_fusion.13
  197.1 1.8 multiply_select_fusion.2
  198.9 2.1 fusion.217
  201.0 4.2 %fusion.218 = f32[4,16,1024]{2,1,0:T(8,128)} fusion(f32[4,16,1024]{2,1,0:T(8,128)} %get-tuple-element.1144, s32[]{:T(128)S(6)} %copy.77, f32[16,1024]{1,0:T(8,128)S(1)} %dynamic-slice_bitcast_fusion.2, f32[1024,1024]{0,1:T(8,128)S(1)} %multiply_select_fusion.2), kind=kOutput, calls=%fused_computation.37.clone.1 | convolution fusion | flops 201326592 | bytes 4325380 | tf_op jit(solution)/shard_map/while/body/eval_jaxpr/dot_general | solution.py:97
  205.2 1.4 fusion.219
  207.7 27.9 %all-gather.21.cloned.1.call-done = f32[16,153,128]{2,1,0:T(8,128)} async-done(((f32[4,153,128]{2,1,0:T(8,128)}), f32[16,153,128]{2,1,0:T(8,128)}) %all-gather.21.cloned.1.call-update) | async-done | bytes 1253392 | tf_op jit(solution)/shard_map/all_gather | solution.py:154
  235.6 2.3 fusion.89
  238.0 8.1 %all-gather.10 = f32[4,4,153]{2,1,0:T(4,128)S(1)} all-gather(f32[1,4,153]{2,1,0:T(4,128)S(1)} %bitcast.303), channel_id=8, replica_groups=mesh['seq'=4,'seg'=4,'head'=2] {'seq'}, dimensions={0}, use_global_device_ids=true | all-gather | bytes 12240 | tf_op jit(solution)/shard_map/all_gather | solution.py:155
  246.2 13.7 %all-gather.11 = f32[4,4,153]{2,1,0:T(4,128)S(1)} all-gather(f32[1,4,153]{2,1,0:T(4,128)S(1)} %bitcast.302), channel_id=9, replica_groups=mesh['seq'=4,'seg'=4,'head'=2] {'seg'}, dimensions={0}, use_global_device_ids=true | all-gather | bytes 12240 | tf_op jit(solution)/shard_map/all_gather | solution.py:13
  259.9 10.9 %all-gather.23.cloned.1.call-done = f32[16,153,128]{2,1,0:T(8,128)} async-done(((f32[4,153,128]{2,1,0:T(8,128)}), f32[16,153,128]{2,1,0:T(8,128)}) %all-gather.23.cloned.1.call-update) | async-done | bytes 1253392 | tf_op jit(solution)/shard_map/all_gather | solution.py:13
  270.8 1.4 rev.6
  272.7 25.7 %while.83 = (s32[]{:T(128)}, f32[4,128,16]{1,2,0:T(8,128)S(1)}, f32[4,128,16]{1,2,0:T(8,128)S(1)}, bf16[4,1024,128]{2,1,0:T(8,128)(2,1)}, bf16[4,16,1024]{2,1,0:...) while((s32[]{:T(128)}, f32[4,128,16]{1,2,0:T(8,128)S(1)}, ...), condition=%wide.region_20.21_spmd.clone, body=%wide.region_19.20_spmd.sunk.clone.sunk | while | flops 156230656 | bytes 5469037 | solution.py:178
  276.8 1.3 fusion.236
  283.2 1.3 fusion.236
  289.6 1.3 fusion.236
  296.0 1.3 fusion.236
  298.4 39.8 %all-reduce = (f32[128,16]{0,1:T(8,128)}, f32[128,16]{0,1:T(8,128)}) all-reduce(f32[128,16]{0,1:T(8,128)S(1)} %reduce_sum.125, f32[128,16]{0,1:T(8,128)S(1)} %reduce_sum.126), channel_id=1, replica_groups=mesh['seq'=4,'seg'=4,'head'=2] {'seq','seg','head'}, use_global_device_ids=true, to_apply=%region_22.23 | all-reduce | flops 4096 | bytes 32768 | tf_op jit(solution)/shard_map/psum | solution.py:182
  (201 shorter events, 62.6 us)
Async XLA Ops:
  7.2 61.0 %all-gather.17.cloned.1.call-start = ((), (), s32[]{:S(2)}) async-start(), calls=%async_computation | async-start | bytes 1638400 | tf_op jit(solution)/shard_map/all_gather | solution.py:154
  35.8 0.7 copy-start.4
  36.6 66.9 %all-gather.19.cloned.1.call-start = ((), (), s32[]{:S(2)}) async-start(), calls=%async_computation.1 | async-start | bytes 1638400 | tf_op jit(solution)/shard_map/all_gather | solution.py:13
  68.1 40.9 %copy-start.2 = (f32[136,16]{1,0:T(8,128)S(1)}, f32[136,16]{1,0:T(8,128)}, u32[]{:S(2)}) copy-start(f32[136,16]{1,0:T(8,128)} %get-tuple-element.1252) | copy-start | bytes 26116
  68.1 40.9 %copy-start.3 = (f32[136,16]{1,0:T(8,128)S(1)}, f32[136,16]{1,0:T(8,128)}, u32[]{:S(2)}) copy-start(f32[136,16]{1,0:T(8,128)} %get-tuple-element.1254) | copy-start | bytes 26116
  68.1 40.9 %copy-start.5 = (f32[136]{0:T(256)S(1)}, f32[136]{0:T(256)}, u32[]{:S(2)}) copy-start(f32[136]{0:T(256)} %get-tuple-element.1271) | copy-start | bytes 1636
  70.5 165.0 %all-gather.21.cloned.1.call-start = ((), (), s32[]{:S(2)}) async-start(), calls=%async_computation.2 | async-start | bytes 1638400 | tf_op jit(solution)/shard_map/all_gather | solution.py:154
  114.3 3.4 copy-start
  119.6 3.9 %copy-start.1 = (f32[1024,1024]{0,1:T(8,128)S(1)}, f32[1024,1024]{0,1:T(8,128)}, u32[]{:S(2)}) copy-start(f32[1024,1024]{0,1:T(8,128)} %copy-done) | copy-start | bytes 12582916 | tf_op jit(solution)/shard_map/while
  123.5 1.9 copy-start.6
  127.4 6.3 %copy-start.7 = (bf16[4,16,1024]{2,1,0:T(8,128)(2,1)}, bf16[4,16,1024]{2,1,0:T(8,128)(2,1)S(1)}, u32[]{:S(2)}) copy-start(bf16[4,16,1024]{2,1,0:T(8,128)(2,1)S(1)} %fusion.217) | copy-start | bytes 393220 | tf_op jit(solution)/shard_map/while
  138.8 3.4 copy-start
  144.1 3.9 %copy-start.1 = (f32[1024,1024]{0,1:T(8,128)S(1)}, f32[1024,1024]{0,1:T(8,128)}, u32[]{:S(2)}) copy-start(f32[1024,1024]{0,1:T(8,128)} %copy-done) | copy-start | bytes 12582916 | tf_op jit(solution)/shard_map/while
  148.0 1.9 copy-start.6
  152.0 6.3 %copy-start.7 = (bf16[4,16,1024]{2,1,0:T(8,128)(2,1)}, bf16[4,16,1024]{2,1,0:T(8,128)(2,1)S(1)}, u32[]{:S(2)}) copy-start(bf16[4,16,1024]{2,1,0:T(8,128)(2,1)S(1)} %fusion.217) | copy-start | bytes 393220 | tf_op jit(solution)/shard_map/while
  163.3 3.4 copy-start
  168.6 3.9 %copy-start.1 = (f32[1024,1024]{0,1:T(8,128)S(1)}, f32[1024,1024]{0,1:T(8,128)}, u32[]{:S(2)}) copy-start(f32[1024,1024]{0,1:T(8,128)} %copy-done) | copy-start | bytes 12582916 | tf_op jit(solution)/shard_map/while
  172.5 1.9 copy-start.6
  176.5 6.3 %copy-start.7 = (bf16[4,16,1024]{2,1,0:T(8,128)(2,1)}, bf16[4,16,1024]{2,1,0:T(8,128)(2,1)S(1)}, u32[]{:S(2)}) copy-start(bf16[4,16,1024]{2,1,0:T(8,128)(2,1)S(1)} %fusion.217) | copy-start | bytes 393220 | tf_op jit(solution)/shard_map/while
  187.8 3.4 copy-start
  193.2 3.9 %copy-start.1 = (f32[1024,1024]{0,1:T(8,128)S(1)}, f32[1024,1024]{0,1:T(8,128)}, u32[]{:S(2)}) copy-start(f32[1024,1024]{0,1:T(8,128)} %copy-done) | copy-start | bytes 12582916 | tf_op jit(solution)/shard_map/while
  197.1 1.9 copy-start.6
  201.0 6.3 %copy-start.7 = (bf16[4,16,1024]{2,1,0:T(8,128)(2,1)}, bf16[4,16,1024]{2,1,0:T(8,128)(2,1)S(1)}, u32[]{:S(2)}) copy-start(bf16[4,16,1024]{2,1,0:T(8,128)(2,1)S(1)} %fusion.217) | copy-start | bytes 393220 | tf_op jit(solution)/shard_map/while
  207.6 63.2 %all-gather.23.cloned.1.call-start = ((), (), s32[]{:S(2)}) async-start(), calls=%async_computation.3 | async-start | bytes 1638400 | tf_op jit(solution)/shard_map/all_gather | solution.py:13
Sparse Core Ops, SparseCore 0:
  36.7 31.3 all-gather.16
  70.7 32.7 all-gather.18
  207.7 27.7 all-gather.20
  238.1 32.7 all-gather.22
where the time goes:
time: 347 us; the launch traced here: 345 us
  matrix products  140 us (40%)
  blocking collectives  83.4 us (24%)
  waiting for transfers between devices  80.6 us (23%)
  between operations  14 us (4%)
  other arithmetic  12.4 us (4%)
  local copies, waits for them, and re-layouts  12.3 us (4%)
    all_gather x2, waiting for transfers between devices, carried(): lax.all_gather(stacked[0], 'seq', axis=0, tiled=True)  59.4 us
    psum x1, blocking collectives, shards(): lax.psum((jnp.sum(grad_q, 0), jnp.sum(grad_k, 0)), ('seq', 'seg', 'head'))  39.8 us
    all_gather x2, blocking collectives, carried_in(): pieces = jax.tree.map(lambda part: lax.all_gather(part, axis), value)  27.4 us
    all_gather x2, waiting for transfers between devices, carried_in(): pieces = jax.tree.map(lambda part: lax.all_gather(part, axis), value)  21.2 us
    dot_general x4, matrix products, head_forward(): g_k = jnp.dot(q_t, g_scores, precision=highest)  16.6 us
    all_gather x2, blocking collectives, carried(): lax.all_gather(stacked[1], 'seq', axis=0, tiled=True)  16.3 us
    dot_general x4, matrix products, head_forward(): lax.dot_general(q_t, k_t, (((0,), (0,)), ((), ())), precision=highest)  15.3 us
    dot_general x8, matrix products, project(): lax.dot_general(weight_b, rows, (((0,), (1,)), ((), ())), preferred_eleme...  9.01 us
  transfers between devices with their start and end apart: 4, of which 4 were waited for; matrix products, arithmetic and copies ran while one was open for 0% of the time, Pallas kernels for 0%

commit v1 on v0

--- a/solution.py
+++ b/solution.py
@@ -6,6 +6,12 @@
 from jax.sharding import PartitionSpec as P
 
 highest = lax.Precision.HIGHEST
+
+
+def pieces_all_expand(page, row_dim):
+    out_arr = list(page.shape[1:])
+    out_arr[row_dim] *= page.shape[0]
+    return jnp.moveaxis(page, 0, row_dim).reshape(out_arr)
 
 
 def carried_in(value, axis, join, neutral, backward):
@@ -146,14 +152,31 @@
 def carried(local, backward):
     zeros = jax.tree.map(jnp.zeros_like, local)
     stacked = jax.tree.map(lambda array: array[None], local)
+
+    def take_spans(in_array, at_axis, a_name):
+        num_devices = jax.lax.axis_size(a_name)
+        by_rank = tuple(((src_i, (src_i + 1) % num_devices) for src_i in range(num_devices)))
+        samples = tuple(((at, d) for d, at in by_rank))
+        right_arr, y = ([], [])
+        for p in range(num_devices - 1):
+            if p % 2 == 0:
+                t_next = jax.lax.ppermute(
+                    right_arr[-1] if right_arr else in_array, axis_name=a_name, perm=by_rank
+                )
+                right_arr.append(t_next)
+            else:
+                y.append(jax.lax.ppermute(y[-1] if y else in_array, axis_name=a_name, perm=samples))
+        base_arr = jnp.stack([*right_arr[::-1], in_array, *y], 0)
+        arr_next = jax.lax.axis_index(a_name)
+        outcome_arr = arr_next - len(right_arr)
+        base_arr = base_arr[(jnp.arange(num_devices) - outcome_arr) % num_devices]
+        return pieces_all_expand(base_arr, at_axis)
+
     inner, totals = masked_fold(
         lax.axis_index("seq"),
         backward,
         (zeros, zeros),
-        (
-            lax.all_gather(stacked[0], "seq", axis=0, tiled=True),
-            lax.all_gather(stacked[1], "seq", axis=0, tiled=True),
-        ),
+        (take_spans(stacked[0], 0, "seq"), lax.all_gather(stacked[1], "seq", axis=0, tiled=True)),
     )
     outer = carried_in(totals, "seg", add_trees, zeros, backward)
     return add_trees(inner, outer)

time: 347 us -> 336 us (0.968)
  waiting for transfers between devices: 80.6 us -> 61.6 us
  starting transfers between devices: 0.16 us -> 8.71 us
    all_gather x2 -> x0, waiting for transfers between devices: 59.4 us -> none  [carried(): lax.all_gather(stacked[0], 'seq', axis=0, tiled=True)]
    ppermute x0 -> x6, waiting for transfers between devices: none -> 41.1 us  [the longest x4 28.2 us: take_spans(): jax.lax.ppermute(right_arr[-1] if right_arr else in_array, axis_name=a_na...]
    ppermute x0 -> x6, starting transfers between devices: none -> 8.63 us  [the longest x4 6.13 us: take_spans(): jax.lax.ppermute(right_arr[-1] if right_arr else in_array, axis_name=a_na...]
  transfers between devices with their start and end apart: 4 -> 8, of which waited for: 4 -> 8; matrix products, arithmetic and copies ran while one was open for 0% -> 0% of each run, Pallas kernels for 0% -> 0%
where the time goes in v1:
time: 336 us; the launch traced here: 334 us
  matrix products  140 us (42%)
  blocking collectives  83.6 us (25%)
  waiting for transfers between devices  61.6 us (18%)
  between operations  14.3 us (4%)
  local copies, waits for them, and re-layouts  12.9 us (4%)
  other arithmetic  10.8 us (3%)
  starting transfers between devices  8.71 us (3%)
    psum x1, blocking collectives, shards(): lax.psum((jnp.sum(grad_q, 0), jnp.sum(grad_k, 0)), ('seq', 'seg', 'head'))  39.8 us
    ppermute x4, waiting for transfers between devices, take_spans(): jax.lax.ppermute(right_arr[-1] if right_arr else in_array, axis_name=a_na...  28.2 us
    all_gather x2, blocking collectives, carried_in(): pieces = jax.tree.map(lambda part: lax.all_gather(part, axis), value)  27.4 us
    all_gather x2, waiting for transfers between devices, carried_in(): pieces = jax.tree.map(lambda part: lax.all_gather(part, axis), value)  20.5 us
    dot_general x4, matrix products, head_forward(): g_k = jnp.dot(q_t, g_scores, precision=highest)  16.8 us
    all_gather x2, blocking collectives, carried(): lax.all_gather(stacked[1], 'seq', axis=0, tiled=True)  16.4 us
    dot_general x4, matrix products, head_forward(): lax.dot_general(q_t, k_t, (((0,), (0,)), ((), ())), precision=highest)  15.2 us
    ppermute x2, waiting for transfers between devices, take_spans(): jax.lax.ppermute(y[-1] if y else in_array, axis_name=a_name, perm=samples)  12.9 us
  transfers between devices with their start and end apart: 8, of which 8 were waited for; matrix products, arithmetic and copies ran while one was open for 0% of the time, Pallas kernels for 0%

profile of v1, /device:TPU:0, one launch (start us, length us, event | category | flops | bytes accessed | tf_op | source)
XLA Modules:
  0.0 333.7 jit_solution(14066489279807718192)
XLA Ops:
  8.7 27.1 %while.81 = (s32[]{:T(128)}, f32[4,16,1024]{2,1,0:T(8,128)S(1)}, f32[4,16,1024]{2,1,0:T(8,128)S(1)}, f32[4,153,128]{2,1,0:T(8,128)S(1)}, f32[4,153]{1,0:T(4,128)...) while((s32[]{:T(128)}, f32[4,16,1024]{2,1,0:T(8,128)S(1)}, ...), condition=%wide.region_2.3_spmd.clone, body=%wide.region_0.2_spmd.sunk.clone.sunk | while | flops 103662440 | bytes 4145861 | solution.py:189
  11.0 1.5 convolution_multiply_fusion.7
  12.5 1.5 fusion.189
  17.7 1.5 convolution_multiply_fusion.7
  19.2 1.5 fusion.189
  24.5 1.5 convolution_multiply_fusion.7
  26.0 1.5 fusion.189
  31.3 1.5 convolution_multiply_fusion.7
  32.8 1.5 fusion.189
  35.8 3.0 collective-permute-start
  39.9 8.5 %collective-permute-done = f32[1,4,153,128]{3,2,1,0:T(8,128)S(1)} collective-permute-done((f32[1,4,153,128]{3,2,1,0:T(8,128)S(1)}, f32[1,4,153,128]{3,2,1,0:T(8,128)S(1)}, u32[]{:S(2)}, u32[]{:S(2)}) %collective-permute-start) | collective-permute-done | bytes 313376 | tf_op jit(solution)/shard_map/ppermute | solution.py:163
  49.5 6.5 %collective-permute-done.2 = f32[1,4,153,128]{3,2,1,0:T(8,128)S(1)} collective-permute-done((f32[1,4,153,128]{3,2,1,0:T(8,128)S(1)}, f32[1,4,153,128]{3,2,1,0:T(8,128)S(1)}, u32[]{:S(2)}, u32[]{:S(2)}) %collective-permute-start.2) | collective-permute-done | bytes 313376 | tf_op jit(solution)/shard_map/ppermute | solution.py:168
  55.9 5.6 %collective-permute-done.1 = f32[1,4,153,128]{3,2,1,0:T(8,128)S(1)} collective-permute-done((f32[1,4,153,128]{3,2,1,0:T(8,128)S(1)}, f32[1,4,153,128]{3,2,1,0:T(8,128)S(1)}, u32[]{:S(2)}, u32[]{:S(2)}) %collective-permute-start.1) | collective-permute-done | bytes 313376 | tf_op jit(solution)/shard_map/ppermute | solution.py:163
  63.4 8.4 %all-gather.6 = f32[4,4,153]{2,1,0:T(4,128)S(1)} all-gather(f32[1,4,153]{2,1,0:T(4,128)S(1)} %bitcast.328), channel_id=3, replica_groups=mesh['seq'=4,'seg'=4,'head'=2] {'seq'}, dimensions={0}, use_global_device_ids=true | all-gather | bytes 12240 | tf_op jit(solution)/shard_map/all_gather | solution.py:179
  71.8 13.8 %all-gather.7 = f32[4,4,153]{2,1,0:T(4,128)S(1)} all-gather(f32[1,4,153]{2,1,0:T(4,128)S(1)} %bitcast.325), channel_id=4, replica_groups=mesh['seq'=4,'seg'=4,'head'=2] {'seg'}, dimensions={0}, use_global_device_ids=true | all-gather | bytes 12240 | tf_op jit(solution)/shard_map/all_gather | solution.py:19
  86.3 10.5 %all-gather.13.cloned.1.call-done = f32[16,153,128]{2,1,0:T(8,128)} async-done(((f32[4,153,128]{2,1,0:T(8,128)}), f32[16,153,128]{2,1,0:T(8,128)}) %all-gather.13.cloned.1.call-update) | async-done | bytes 1253392 | tf_op jit(solution)/shard_map/all_gather | solution.py:19
  96.7 3.4 %while.84 = (s32[]{:T(128)}, f32[4,153,128]{2,1,0:T(8,128)S(1)}, f32[4,153]{1,0:T(4,128)S(1)}, s32[]{:T(128)}, f32[4,4,153,128]{3,2,1,0:T(8,128)}, /*index=5*/f32[4,4,153]{2,1,0:T(4,128)S(1)}, s32[]{:T(128)}, s32[]{:T(128)}) while((s32[]{:T(128)}, f32[4,153,128]{2,1,0:T(8,128)S(1)}, f32[4,153]{1,0:T(4,128)S(1)}, s32[]{:T(128)}, ...), condition=%wide.region_7.8_spmd.clone, body=%wide.region_6.7_spmd.clone.sunk | while | flops 236848 | bytes 947499 | solution.py:31
  102.4 98.6 %while.82 = (s32[]{:T(128)}, bf16[4,1024,128]{2,1,0:T(8,128)(2,1)}, bf16[4,16,1024]{2,1,0:T(8,128)(2,1)}, f32[4,16,1024]{2,1,0:T(8,128)}, f32[4,153,128]{2,1,0:T...) while((s32[]{:T(128)}, bf16[4,1024,128]{2,1,0:T(8,128)(2,1)}, ...), condition=%wide.region_12.13_spmd.clone, body=%wide.region_9.12_spmd.sunk.clone.sunk | while | flops 1998507008 | bytes 75882544 | solution.py:196
  103.7 3.8 %fusion.214 = (f32[1024]{0:T(1024)S(1)}, f32[1024,1024]{0,1:T(8,128)S(1)}) fusion(f32[16,1024]{1,0:T(8,128)S(1)} %dynamic-slice_bitcast_fusion.2, f32[4,16,1024]{2,1,0:T(8,128)S(1)} %get-tuple-element.1167, s32[]{:T(128)S(6)} %copy.77), kind=kOutput, calls=%fused_computation.30.clone.1 | convolution fusion | flops 208665600 | bytes 4329476 | tf_op jit(solution)/shard_map/while/body/eval_jaxpr/dot_general | solution.py:82
  109.3 1.6 fusion.217
  110.9 1.8 fusion.218
  113.6 2.1 convolution_add_fusion.13
  116.8 1.8 multiply_select_fusion.2
  118.6 2.1 fusion.219
  120.7 4.2 %fusion.220 = f32[4,16,1024]{2,1,0:T(8,128)} fusion(f32[4,16,1024]{2,1,0:T(8,128)} %get-tuple-element.1144, s32[]{:T(128)S(6)} %copy.77, f32[16,1024]{1,0:T(8,128)S(1)} %dynamic-slice_bitcast_fusion.2, f32[1024,1024]{0,1:T(8,128)S(1)} %multiply_select_fusion.2), kind=kOutput, calls=%fused_computation.39.clone.1 | convolution fusion | flops 201326592 | bytes 4325380 | tf_op jit(solution)/shard_map/while/body/eval_jaxpr/dot_general | solution.py:103
  124.9 1.4 fusion.221
  128.3 3.8 %fusion.214 = (f32[1024]{0:T(1024)S(1)}, f32[1024,1024]{0,1:T(8,128)S(1)}) fusion(f32[16,1024]{1,0:T(8,128)S(1)} %dynamic-slice_bitcast_fusion.2, f32[4,16,1024]{2,1,0:T(8,128)S(1)} %get-tuple-element.1167, s32[]{:T(128)S(6)} %copy.77), kind=kOutput, calls=%fused_computation.30.clone.1 | convolution fusion | flops 208665600 | bytes 4329476 | tf_op jit(solution)/shard_map/while/body/eval_jaxpr/dot_general | solution.py:82
  133.9 1.6 fusion.217
  135.5 1.8 fusion.218
  138.1 2.1 convolution_add_fusion.13
  141.3 1.8 multiply_select_fusion.2
  143.2 2.1 fusion.219
  145.3 4.2 %fusion.220 = f32[4,16,1024]{2,1,0:T(8,128)} fusion(f32[4,16,1024]{2,1,0:T(8,128)} %get-tuple-element.1144, s32[]{:T(128)S(6)} %copy.77, f32[16,1024]{1,0:T(8,128)S(1)} %dynamic-slice_bitcast_fusion.2, f32[1024,1024]{0,1:T(8,128)S(1)} %multiply_select_fusion.2), kind=kOutput, calls=%fused_computation.39.clone.1 | convolution fusion | flops 201326592 | bytes 4325380 | tf_op jit(solution)/shard_map/while/body/eval_jaxpr/dot_general | solution.py:103
  149.5 1.4 fusion.221
  152.8 3.8 %fusion.214 = (f32[1024]{0:T(1024)S(1)}, f32[1024,1024]{0,1:T(8,128)S(1)}) fusion(f32[16,1024]{1,0:T(8,128)S(1)} %dynamic-slice_bitcast_fusion.2, f32[4,16,1024]{2,1,0:T(8,128)S(1)} %get-tuple-element.1167, s32[]{:T(128)S(6)} %copy.77), kind=kOutput, calls=%fused_computation.30.clone.1 | convolution fusion | flops 208665600 | bytes 4329476 | tf_op jit(solution)/shard_map/while/body/eval_jaxpr/dot_general | solution.py:82
  158.4 1.6 fusion.217
  160.0 1.8 fusion.218
  162.7 2.1 convolution_add_fusion.13
  165.9 1.8 multiply_select_fusion.2
  167.7 2.1 fusion.219
  169.8 4.2 %fusion.220 = f32[4,16,1024]{2,1,0:T(8,128)} fusion(f32[4,16,1024]{2,1,0:T(8,128)} %get-tuple-element.1144, s32[]{:T(128)S(6)} %copy.77, f32[16,1024]{1,0:T(8,128)S(1)} %dynamic-slice_bitcast_fusion.2, f32[1024,1024]{0,1:T(8,128)S(1)} %multiply_select_fusion.2), kind=kOutput, calls=%fused_computation.39.clone.1 | convolution fusion | flops 201326592 | bytes 4325380 | tf_op jit(solution)/shard_map/while/body/eval_jaxpr/dot_general | solution.py:103
  174.0 1.4 fusion.221
  177.4 3.8 %fusion.214 = (f32[1024]{0:T(1024)S(1)}, f32[1024,1024]{0,1:T(8,128)S(1)}) fusion(f32[16,1024]{1,0:T(8,128)S(1)} %dynamic-slice_bitcast_fusion.2, f32[4,16,1024]{2,1,0:T(8,128)S(1)} %get-tuple-element.1167, s32[]{:T(128)S(6)} %copy.77), kind=kOutput, calls=%fused_computation.30.clone.1 | convolution fusion | flops 208665600 | bytes 4329476 | tf_op jit(solution)/shard_map/while/body/eval_jaxpr/dot_general | solution.py:82
  182.9 1.6 fusion.217
  184.5 1.8 fusion.218
  187.2 2.1 convolution_add_fusion.13
  190.4 1.8 multiply_select_fusion.2
  192.2 2.1 fusion.219
  194.3 4.2 %fusion.220 = f32[4,16,1024]{2,1,0:T(8,128)} fusion(f32[4,16,1024]{2,1,0:T(8,128)} %get-tuple-element.1144, s32[]{:T(128)S(6)} %copy.77, f32[16,1024]{1,0:T(8,128)S(1)} %dynamic-slice_bitcast_fusion.2, f32[1024,1024]{0,1:T(8,128)S(1)} %multiply_select_fusion.2), kind=kOutput, calls=%fused_computation.39.clone.1 | convolution fusion | flops 201326592 | bytes 4325380 | tf_op jit(solution)/shard_map/while/body/eval_jaxpr/dot_general | solution.py:103
  198.5 1.4 fusion.221
  200.9 1.5 collective-permute-start.3
  202.4 1.5 collective-permute-start.5
  203.9 8.8 %collective-permute-done.3 = f32[1,4,153,128]{3,2,1,0:T(8,128)S(1)} collective-permute-done((f32[1,4,153,128]{3,2,1,0:T(8,128)}, f32[1,4,153,128]{3,2,1,0:T(8,128)S(1)}, u32[]{:S(2)}, u32[]{:S(2)}) %collective-permute-start.3) | collective-permute-done | bytes 313376 | tf_op jit(solution)/shard_map/ppermute | solution.py:163
  213.2 6.5 %collective-permute-done.5 = f32[1,4,153,128]{3,2,1,0:T(8,128)S(1)} collective-permute-done((f32[1,4,153,128]{3,2,1,0:T(8,128)}, f32[1,4,153,128]{3,2,1,0:T(8,128)S(1)}, u32[]{:S(2)}, u32[]{:S(2)}) %collective-permute-start.5) | collective-permute-done | bytes 313376 | tf_op jit(solution)/shard_map/ppermute | solution.py:168
  219.7 5.3 %collective-permute-done.4 = f32[1,4,153,128]{3,2,1,0:T(8,128)S(1)} collective-permute-done((f32[1,4,153,128]{3,2,1,0:T(8,128)S(1)}, f32[1,4,153,128]{3,2,1,0:T(8,128)S(1)}, u32[]{:S(2)}, u32[]{:S(2)}) %collective-permute-start.4) | collective-permute-done | bytes 313376 | tf_op jit(solution)/shard_map/ppermute | solution.py:163
  227.7 8.1 %all-gather.8 = f32[4,4,153]{2,1,0:T(4,128)S(1)} all-gather(f32[1,4,153]{2,1,0:T(4,128)S(1)} %bitcast.327), channel_id=6, replica_groups=mesh['seq'=4,'seg'=4,'head'=2] {'seq'}, dimensions={0}, use_global_device_ids=true | all-gather | bytes 12240 | tf_op jit(solution)/shard_map/all_gather | solution.py:179
  235.8 13.6 %all-gather.9 = f32[4,4,153]{2,1,0:T(4,128)S(1)} all-gather(f32[1,4,153]{2,1,0:T(4,128)S(1)} %bitcast.326), channel_id=7, replica_groups=mesh['seq'=4,'seg'=4,'head'=2] {'seg'}, dimensions={0}, use_global_device_ids=true | all-gather | bytes 12240 | tf_op jit(solution)/shard_map/all_gather | solution.py:19
  249.5 10.1 %all-gather.15.cloned.1.call-done = f32[16,153,128]{2,1,0:T(8,128)} async-done(((f32[4,153,128]{2,1,0:T(8,128)}), f32[16,153,128]{2,1,0:T(8,128)}) %all-gather.15.cloned.1.call-update) | async-done | bytes 1253392 | tf_op jit(solution)/shard_map/all_gather | solution.py:19
  259.5 1.4 rev.6
  261.4 25.7 %while.83 = (s32[]{:T(128)}, f32[4,128,16]{1,2,0:T(8,128)S(1)}, f32[4,128,16]{1,2,0:T(8,128)S(1)}, bf16[4,1024,128]{2,1,0:T(8,128)(2,1)}, bf16[4,16,1024]{2,1,0:...) while((s32[]{:T(128)}, f32[4,128,16]{1,2,0:T(8,128)S(1)}, ...), condition=%wide.region_20.21_spmd.clone, body=%wide.region_19.20_spmd.sunk.clone.sunk | while | flops 156230656 | bytes 5469037 | solution.py:201
  265.5 1.3 fusion.238
  271.9 1.3 fusion.238
  278.3 1.3 fusion.238
  287.1 39.8 %all-reduce = (f32[128,16]{0,1:T(8,128)}, f32[128,16]{0,1:T(8,128)}) all-reduce(f32[128,16]{0,1:T(8,128)S(1)} %reduce_sum.125, f32[128,16]{0,1:T(8,128)S(1)} %reduce_sum.126), channel_id=1, replica_groups=mesh['seq'=4,'seg'=4,'head'=2] {'seq','seg','head'}, use_global_device_ids=true, to_apply=%region_22.23 | all-reduce | flops 4096 | bytes 32768 | tf_op jit(solution)/shard_map/psum | solution.py:205
  (211 shorter events, 75.0 us)
Async XLA Ops:
  7.2 89.6 %all-gather.13.cloned.1.call-start = ((), (), s32[]{:S(2)}) async-start(), calls=%async_computation | async-start | bytes 1638400 | tf_op jit(solution)/shard_map/all_gather | solution.py:19
  35.8 12.5 %collective-permute-start = (f32[1,4,153,128]{3,2,1,0:T(8,128)S(1)}, f32[1,4,153,128]{3,2,1,0:T(8,128)S(1)}, u32[]{:S(2)}, u32[]{:S(2)}) collective-permute-start(f32[1,4,153,128]{3,2,1,0:T(8,128)S(1)} %bitcast.310), channel_id=1, source_target_pairs={{0,8},{8,16},{16,24},{24,0},{1,9},{9,17},{17,25},{25,1},{2,10},{10... | collective-permute-start | bytes 940040 | tf_op jit(solution)/shard_map/ppermute | solution.py:163
  38.8 17.1 %collective-permute-start.2 = (f32[1,4,153,128]{3,2,1,0:T(8,128)S(1)}, f32[1,4,153,128]{3,2,1,0:T(8,128)S(1)}, u32[]{:S(2)}, u32[]{:S(2)}) collective-permute-start(f32[1,4,153,128]{3,2,1,0:T(8,128)S(1)} %bitcast.311), channel_id=1, source_target_pairs={{8,0},{16,8},{24,16},{0,24},{9,1},{17,9},{25,17},{1,25},{10,2},{18... | collective-permute-start | bytes 940040 | tf_op jit(solution)/shard_map/ppermute | solution.py:168
  48.3 13.2 %collective-permute-start.1 = (f32[1,4,153,128]{3,2,1,0:T(8,128)S(1)}, f32[1,4,153,128]{3,2,1,0:T(8,128)S(1)}, u32[]{:S(2)}, u32[]{:S(2)}) collective-permute-start(f32[1,4,153,128]{3,2,1,0:T(8,128)S(1)} %collective-permute-done), channel_id=1, source_target_pairs={{0,8},{8,16},{16,24},{24,0},{1,9},{9,17},{17,25},{25,1},{2,10},{10... | collective-permute-start | bytes 940040 | tf_op jit(solution)/shard_map/ppermute | solution.py:163
  62.3 40.1 %copy-start.2 = (f32[136,16]{1,0:T(8,128)S(1)}, f32[136,16]{1,0:T(8,128)}, u32[]{:S(2)}) copy-start(f32[136,16]{1,0:T(8,128)} %get-tuple-element.1250) | copy-start | bytes 26116
  62.3 40.1 %copy-start.3 = (f32[136,16]{1,0:T(8,128)S(1)}, f32[136,16]{1,0:T(8,128)}, u32[]{:S(2)}) copy-start(f32[136,16]{1,0:T(8,128)} %get-tuple-element.1252) | copy-start | bytes 26116
  62.3 40.1 %copy-start.4 = (f32[136]{0:T(256)S(1)}, f32[136]{0:T(256)}, u32[]{:S(2)}) copy-start(f32[136]{0:T(256)} %get-tuple-element.1267) | copy-start | bytes 1636
  63.3 196.2 %all-gather.15.cloned.1.call-start = ((), (), s32[]{:S(2)}) async-start(), calls=%async_computation.1 | async-start | bytes 1638400 | tf_op jit(solution)/shard_map/all_gather | solution.py:19
  107.5 3.4 %copy-start = (f32[1024,1024]{0,1:T(8,128)}, f32[1024,1024]{0,1:T(8,128)S(1)}, u32[]{:S(2)}) copy-start(f32[1024,1024]{0,1:T(8,128)S(1)} %get-tuple-element.1020) | copy-start | bytes 12582916 | tf_op jit(solution)/shard_map/while
  112.9 3.9 %copy-start.1 = (f32[1024,1024]{0,1:T(8,128)S(1)}, f32[1024,1024]{0,1:T(8,128)}, u32[]{:S(2)}) copy-start(f32[1024,1024]{0,1:T(8,128)} %copy-done) | copy-start | bytes 12582916 | tf_op jit(solution)/shard_map/while
  116.8 1.9 copy-start.5
  120.7 6.4 %copy-start.6 = (bf16[4,16,1024]{2,1,0:T(8,128)(2,1)}, bf16[4,16,1024]{2,1,0:T(8,128)(2,1)S(1)}, u32[]{:S(2)}) copy-start(bf16[4,16,1024]{2,1,0:T(8,128)(2,1)S(1)} %fusion.219) | copy-start | bytes 393220 | tf_op jit(solution)/shard_map/while
  132.1 3.4 %copy-start = (f32[1024,1024]{0,1:T(8,128)}, f32[1024,1024]{0,1:T(8,128)S(1)}, u32[]{:S(2)}) copy-start(f32[1024,1024]{0,1:T(8,128)S(1)} %get-tuple-element.1020) | copy-start | bytes 12582916 | tf_op jit(solution)/shard_map/while
  137.4 3.9 %copy-start.1 = (f32[1024,1024]{0,1:T(8,128)S(1)}, f32[1024,1024]{0,1:T(8,128)}, u32[]{:S(2)}) copy-start(f32[1024,1024]{0,1:T(8,128)} %copy-done) | copy-start | bytes 12582916 | tf_op jit(solution)/shard_map/while
  141.3 1.9 copy-start.5
  145.3 6.4 %copy-start.6 = (bf16[4,16,1024]{2,1,0:T(8,128)(2,1)}, bf16[4,16,1024]{2,1,0:T(8,128)(2,1)S(1)}, u32[]{:S(2)}) copy-start(bf16[4,16,1024]{2,1,0:T(8,128)(2,1)S(1)} %fusion.219) | copy-start | bytes 393220 | tf_op jit(solution)/shard_map/while
  156.6 3.4 %copy-start = (f32[1024,1024]{0,1:T(8,128)}, f32[1024,1024]{0,1:T(8,128)S(1)}, u32[]{:S(2)}) copy-start(f32[1024,1024]{0,1:T(8,128)S(1)} %get-tuple-element.1020) | copy-start | bytes 12582916 | tf_op jit(solution)/shard_map/while
  161.9 3.9 %copy-start.1 = (f32[1024,1024]{0,1:T(8,128)S(1)}, f32[1024,1024]{0,1:T(8,128)}, u32[]{:S(2)}) copy-start(f32[1024,1024]{0,1:T(8,128)} %copy-done) | copy-start | bytes 12582916 | tf_op jit(solution)/shard_map/while
  165.8 1.9 copy-start.5
  169.8 6.4 %copy-start.6 = (bf16[4,16,1024]{2,1,0:T(8,128)(2,1)}, bf16[4,16,1024]{2,1,0:T(8,128)(2,1)S(1)}, u32[]{:S(2)}) copy-start(bf16[4,16,1024]{2,1,0:T(8,128)(2,1)S(1)} %fusion.219) | copy-start | bytes 393220 | tf_op jit(solution)/shard_map/while
  181.2 3.4 %copy-start = (f32[1024,1024]{0,1:T(8,128)}, f32[1024,1024]{0,1:T(8,128)S(1)}, u32[]{:S(2)}) copy-start(f32[1024,1024]{0,1:T(8,128)S(1)} %get-tuple-element.1020) | copy-start | bytes 12582916 | tf_op jit(solution)/shard_map/while
  186.5 3.9 %copy-start.1 = (f32[1024,1024]{0,1:T(8,128)S(1)}, f32[1024,1024]{0,1:T(8,128)}, u32[]{:S(2)}) copy-start(f32[1024,1024]{0,1:T(8,128)} %copy-done) | copy-start | bytes 12582916 | tf_op jit(solution)/shard_map/while
  190.4 1.9 copy-start.5
  194.3 6.4 %copy-start.6 = (bf16[4,16,1024]{2,1,0:T(8,128)(2,1)}, bf16[4,16,1024]{2,1,0:T(8,128)(2,1)S(1)}, u32[]{:S(2)}) copy-start(bf16[4,16,1024]{2,1,0:T(8,128)(2,1)S(1)} %fusion.219) | copy-start | bytes 393220 | tf_op jit(solution)/shard_map/while
  200.9 11.7 %collective-permute-start.3 = (f32[1,4,153,128]{3,2,1,0:T(8,128)}, f32[1,4,153,128]{3,2,1,0:T(8,128)S(1)}, u32[]{:S(2)}, u32[]{:S(2)}) collective-permute-start(f32[1,4,153,128]{3,2,1,0:T(8,128)} %bitcast.307), channel_id=1, source_target_pairs={{0,8},{8,16},{16,24},{24,0},{1,9},{9,17},{17,25},{25,1},{2,10},{10... | collective-permute-start | bytes 940040 | tf_op jit(solution)/shard_map/ppermute | solution.py:163
  202.4 17.3 %collective-permute-start.5 = (f32[1,4,153,128]{3,2,1,0:T(8,128)}, f32[1,4,153,128]{3,2,1,0:T(8,128)S(1)}, u32[]{:S(2)}, u32[]{:S(2)}) collective-permute-start(f32[1,4,153,128]{3,2,1,0:T(8,128)} %bitcast.308), channel_id=1, source_target_pairs={{8,0},{16,8},{24,16},{0,24},{9,1},{17,9},{25,17},{1,25},{10,2},{18... | collective-permute-start | bytes 940040 | tf_op jit(solution)/shard_map/ppermute | solution.py:168
  212.7 12.3 %collective-permute-start.4 = (f32[1,4,153,128]{3,2,1,0:T(8,128)S(1)}, f32[1,4,153,128]{3,2,1,0:T(8,128)S(1)}, u32[]{:S(2)}, u32[]{:S(2)}) collective-permute-start(f32[1,4,153,128]{3,2,1,0:T(8,128)S(1)} %collective-permute-done.3), channel_id=1, source_target_pairs={{0,8},{8,16},{16,24},{24,0},{1,9},{9,17},{17,25},{25,1},{2,10},{10... | collective-permute-start | bytes 940040 | tf_op jit(solution)/shard_map/ppermute | solution.py:163
Sparse Core Ops, SparseCore 0:
  63.4 33.2 all-gather.12
  227.8 31.7 all-gather.14
